TPU v7x, 32 devices: a whole 2x2x4 slice. The times are simulated.
32 devices in a mesh: var: 8 (over z, core), samp: 4 (over y, x).
Axes of the slice: x: 2, y: 2, z: 4, core: 2. Of those that a mesh axis runs over, the one named last changes fastest.
Arguments:
- geno: bfloat16 [8192, 16384], P('samp', 'var'), may hold values from -5 to 5
- scale_index: int32 [64, 16384], P('samp', 'var'), may hold values from 0 to 15
- scale_table: float32 [16], replicated, may hold values from 0.25 to 4
- residual: float32 [8, 8192], P(None, 'samp'), may hold values from -6 to 6
- beta_active: float32 [8, 3584], P(None, 'var'), may hold values from -6 to 6
- block_inverse: float32 [16, 256, 256], P('var'), may hold values from -1 to 4
- active_ids: int32 [3584], P('var'), may hold values from 0 to 16383, as said below
- admit_ids: int32 [512], P('var'), may hold values from 0 to 16383, as said below
Outputs:
- scores: float32 [8, 16384], P(None, 'var')
- coefficients: float32 [8, 4096], P(None, 'var')
- residual_out: float32 [8, 8192], P(None, 'samp')
Inputs may be any that keep to these rules, and one draw needn't show every extreme that they name: Variant ids, all different from one another and from those of admit_ids. The fitting slots of one index of var are its 448 entries of active_ids followed by its 64 entries of admit_ids; of these 512 slots at most 128 name variants held by any one index of var, and for every index of var some one holder reaches exactly 128. `admit_ids`: variant ids, as for active_ids.
All inputs are finite; a program needn't handle non-finite values.
Results may differ from a plain program's by a relative error of at most 0.004.
Values may be sent and summed in bfloat16 or wider, within the bound.
A program may use at most 128 MiB of HBM per device.

v0:
```python
import math
import jax
import jax.numpy as jnp
from jax import lax
from jax.sharding import PartitionSpec as P

PASSES = 3
penalty = 0.5
epsilon = 1e-06


def dequantize(values, indices, lookup):
    levels = lookup.shape[0]
    onehot = (indices[:, :, None] == jnp.arange(levels, dtype=jnp.int32)).astype(jnp.float32)
    scales = jnp.dot(onehot, lookup, precision=lax.Precision.HIGHEST)
    groups = indices.shape[0]
    widened = (
        values.reshape(groups, values.shape[0] // groups, values.shape[1]).astype(jnp.float32)
        * scales[:, None, :]
    )
    return widened.reshape(values.shape).astype(jnp.bfloat16)


def slot_layout(variant_ids, var_width, var_count):
    holder = variant_ids // var_width
    column = variant_ids % var_width
    owner_marks = (holder[..., None] == jnp.arange(var_count, dtype=jnp.int32)).astype(jnp.int32)
    before = jnp.cumsum(owner_marks, axis=-2) - owner_marks
    serial = jnp.sum(before * owner_marks, -1)
    return (holder, column, serial)


def block_update(gradient, coeffs, inverse):
    phenos, fit_width = gradient.shape
    blocks, block_size = (inverse.shape[0], inverse.shape[1])
    inner_term = (gradient - penalty * coeffs).reshape(phenos, blocks, block_size)
    direction = jnp.einsum("bij,pbj->pbi", inverse, inner_term, precision=lax.Precision.HIGHEST)
    return direction.reshape(phenos, fit_width).astype(jnp.bfloat16)


def on_device(
    geno, scale_index, scale_table, residual, beta_active, block_inverse, active_ids, admit_ids
):
    var_count = lax.axis_size("var")
    var_rank = lax.axis_index("var")
    samp_rows, var_width = geno.shape
    inv_root = 1.0 / math.sqrt(samp_rows * lax.axis_size("samp"))
    phenos = residual.shape[0]
    local_ids = jnp.concatenate([active_ids, admit_ids])
    fit_width = local_ids.shape[0]
    capacity = 2 * fit_width // var_count
    dequant = dequantize(geno, scale_index, scale_table)
    resid_low = residual.astype(jnp.bfloat16)
    screened = (
        lax.psum(jnp.dot(resid_low, dequant, preferred_element_type=jnp.float32), "samp") * inv_root
    )
    all_ids = lax.all_gather(local_ids, "var", axis=0, tiled=True).reshape(var_count, fit_width)
    holder, column, serial = slot_layout(all_ids, var_width, var_count)
    held_here = holder == var_rank
    wanted = held_here[:, None, :] & (
        serial[:, None, :] == jnp.arange(capacity, dtype=jnp.int32)[None, :, None]
    )
    source_column = jnp.sum(jnp.where(wanted, column[:, None, :], 0), -1).reshape(-1)
    present = jnp.any(wanted, -1).reshape(-1)
    selected = jnp.where(
        present[None, :], jnp.take(dequant, source_column, axis=1), jnp.zeros((), jnp.bfloat16)
    )
    position = lax.dynamic_index_in_dim(holder * capacity + serial, var_rank, 0, keepdims=False)
    coeffs = jnp.concatenate([beta_active, jnp.zeros((phenos, admit_ids.shape[0]), jnp.float32)], 1)
    current = residual
    for pass_index in range(PASSES):
        partial_sums = lax.psum(
            jnp.dot(resid_low, selected, preferred_element_type=jnp.float32), "samp"
        )
        routed = lax.all_to_all(partial_sums, "var", split_axis=1, concat_axis=1, tiled=True)
        gradient = jnp.take(routed, position, axis=1) * inv_root
        direction = block_update(gradient, coeffs, block_inverse)
        placed = (
            jnp.zeros((phenos, var_count * capacity), jnp.bfloat16).at[:, position].set(direction)
        )
        returned = lax.all_to_all(placed, "var", split_axis=1, concat_axis=1, tiled=True)
        partial_update = jnp.einsum(
            "pc,sc->ps", returned, selected, preferred_element_type=jnp.float32
        )
        update = lax.psum(partial_update, "var") * inv_root
        cross_sum, square = lax.psum(
            (jnp.sum(current * update, 1), jnp.sum(update * update, 1)), "samp"
        )
        factor = (cross_sum / (square + epsilon))[:, None]
        current = current - factor * update
        coeffs = coeffs + factor * direction.astype(jnp.float32)
        if pass_index + 1 < PASSES:
            resid_low = current.astype(jnp.bfloat16)
    return (screened, coeffs, current)


def solution(mesh):
    placed = (
        P("samp", "var"),
        P("samp", "var"),
        P(),
        P(None, "samp"),
        P(None, "var"),
        P("var", None, None),
        P("var"),
        P("var"),
    )
    return jax.shard_map(
        on_device,
        mesh=mesh,
        in_specs=placed,
        out_specs=(P(None, "var"), P(None, "var"), P(None, "samp")),
        check_vma=False,
    )
```

profile of v0, /device:TPU:0, one launch (start us, length us, event | category | flops | bytes accessed | tf_op | source)
XLA Modules:
  0.0 450.3 jit_solution(15364064158792349478)
XLA Ops:
  8.0 1.7 fusion.3
  9.7 0.3 copy.93
  10.1 12.3 %copy.78 = bf16[2048,2048]{0,1:T(8,128)(2,1)} copy(bf16[2048,2048]{1,0:T(8,128)(2,1)} %param.10) | data formatting | bytes 16777216 | tf_op args[0]
  22.5 14.5 %all-gather = s32[8,1,512]{2,1,0:T(1,128)S(1)} all-gather(s32[1,1,512]{2,1,0:T(1,128)S(1)} %bitcast.157), channel_id=1, replica_groups=mesh['var'=8,'samp'=4] {'var'}, dimensions={0}, use_global_device_ids=true | all-gather | bytes 18432 | tf_op jit(solution)/shard_map/all_gather | solution.py:57
  37.0 9.0 %reduce-window.6 = s32[8,8,4,128]{3,1,2,0:T(8,128)S(1)} reduce-window(s32[8,8,4,128]{3,1,2,0:T(8,128)S(1)} %fusion.13, s32[]{:T(128)} %constant.73.clone.1), window={size=1x1x1x128 pad=0_0x0_0x0_0x127_0}, to_apply=%region_1.2 | reduce-window | flops 4161536 | bytes 262148 | tf_op jit(solution)/shard_map/reduce-window
  46.1 0.3 copy.79
  46.6 0.1 fusion.6
  46.7 0.4 fusion.2
  47.1 0.5 select_reduce_fusion
  47.6 4.6 %mul.124 = f32[16,128,2048]{1,0,2:T(8,128)S(1)} broadcast(f32[16,2048]{0,1:T(8,128)S(1)} %bitcast.133), dimensions={0,2} | broadcast | bytes 16908288 | tf_op jit(solution)/shard_map/mul | solution.py:18
  52.2 9.2 %fusion = bf16[2048,2048]{0,1:T(8,128)(2,1)} fusion(f32[256,8,16,128]{3,2,1,0:T(8,128)S(1)} %bitcast.130, bf16[2048,2048]{0,1:T(8,128)(2,1)S(1)} %bitcast.132), kind=kLoop, calls=%fused_computation.8 | loop fusion | flops 12582912 | bytes 33554432 | tf_op jit(solution)/shard_map/convert_element_type | solution.py:21
  61.4 13.3 %gather_fusion = bf16[1024,2048]{1,0:T(8,128)(2,1)} fusion(bf16[2048,2048]{0,1:T(8,128)(2,1)} %fusion, s32[1024]{0:T(1024)S(1)} %broadcast_clamp_fusion), kind=kCustom, calls=%fused_computation.3 | custom fusion | bytes 8392704 | tf_op jit(solution)/shard_map/jit(_take)/gather | solution.py:66
  74.7 2.8 select_select_fusion
  77.5 2.0 copy-done.1
  79.5 1.2 convolution_bitcast_fusion.3
  80.6 16.9 %psum.92 = f32[8,8,128]{2,0,1:T(8,128)} all-reduce(f32[8,8,128]{2,0,1:T(8,128)S(1)} %convolution_bitcast_fusion.3), channel_id=1, replica_groups=mesh['var'=8,'samp'=4] {'samp'}, use_global_device_ids=true, to_apply=%region_6.7 | all-reduce | flops 8192 | bytes 65536 | tf_op jit(solution)/shard_map/psum | solution.py:72
  97.5 3.4 all-to-all-start
  100.9 0.2 all-reduce.11.cloned.1.call-start
  101.2 5.5 %all-to-all-done = f32[8,8,128]{2,0,1:T(8,128)S(1)} async-done(((f32[8,8,128]{2,0,1:T(8,128)}), f32[8,8,128]{2,0,1:T(8,128)S(1)}, u32[]{:S(2)}, u32[]{:S(2)}) %all-to-all-start) | async-done | bytes 32800 | tf_op jit(solution)/shard_map/all_to_all | solution.py:75
  106.6 0.2 copy.81
  106.8 1.0 gather_fusion.1
  108.0 0.5 convolution_convert_fusion.2
  108.5 0.2 copy.83
  108.7 1.8 scatter_custom_fusion
  110.7 8.0 %all_to_all.72 = bf16[8,8,128]{2,0,1:T(8,128)(2,1)S(1)} all-to-all(bf16[8,8,128]{2,0,1:T(8,128)(2,1)S(1)} %copy.84), channel_id=1, replica_groups=mesh['var'=8,'samp'=4] {'var'}, dimensions={1} | all-to-all | bytes 32768 | tf_op jit(solution)/shard_map/all_to_all | solution.py:81
  118.7 3.5 fusion.24
  122.2 51.3 %all-reduce.11.cloned.1.call-done = f32[8,2048]{1,0:T(8,128)} async-done(((f32[8,2048]{1,0:T(8,128)}), f32[8,2048]{1,0:T(8,128)}) %all-reduce.11.cloned.1.call-update) | async-done | bytes 65552 | tf_op jit(solution)/shard_map/psum | solution.py:85
  173.5 1.0 multiply_reduce_fusion.4
  174.5 9.8 %all-reduce.3 = (f32[8]{0:T(128)S(1)}, f32[8]{0:T(128)S(1)}) all-reduce(f32[8]{0:T(128)S(1)} %get-tuple-element.21, f32[8]{0:T(128)S(1)} %get-tuple-element.20), channel_id=1, replica_groups=mesh['var'=8,'samp'=4] {'samp'}, use_global_device_ids=true, to_apply=%region_10.12 | all-reduce | flops 16 | bytes 128 | tf_op jit(solution)/shard_map/psum | solution.py:86
  184.4 0.9 multiply_subtract_fusion.2
  185.3 3.4 convolution_bitcast_fusion.2
  188.7 14.4 %psum.96 = f32[8,8,128]{2,0,1:T(8,128)S(1)} all-reduce(f32[8,8,128]{2,0,1:T(8,128)S(1)} %convolution_bitcast_fusion.2), channel_id=1, replica_groups=mesh['var'=8,'samp'=4] {'samp'}, use_global_device_ids=true, to_apply=%region_13.15 | all-reduce | flops 8192 | bytes 65536 | tf_op jit(solution)/shard_map/psum | solution.py:72
  203.0 8.3 %all_to_all.73 = f32[8,8,128]{2,0,1:T(8,128)S(1)} all-to-all(f32[8,8,128]{2,0,1:T(8,128)S(1)} %psum.96), channel_id=1, replica_groups=mesh['var'=8,'samp'=4] {'var'}, dimensions={1} | all-to-all | bytes 65536 | tf_op jit(solution)/shard_map/all_to_all | solution.py:75
  211.3 0.2 copy.85
  211.5 1.0 gather_fusion.2
  212.8 0.5 convolution_convert_fusion.1
  213.3 0.2 copy.87
  213.5 1.8 scatter_custom_fusion.1
  215.4 8.0 %all_to_all.74 = bf16[8,8,128]{2,0,1:T(8,128)(2,1)S(1)} all-to-all(bf16[8,8,128]{2,0,1:T(8,128)(2,1)S(1)} %copy.88), channel_id=1, replica_groups=mesh['var'=8,'samp'=4] {'var'}, dimensions={1} | all-to-all | bytes 32768 | tf_op jit(solution)/shard_map/all_to_all | solution.py:81
  223.4 3.5 fusion.21
  226.9 52.2 %all-reduce.13.cloned.1.call-done = f32[8,2048]{1,0:T(8,128)} async-done(((f32[8,2048]{1,0:T(8,128)}), f32[8,2048]{1,0:T(8,128)}) %all-reduce.13.cloned.1.call-update) | async-done | bytes 65552 | tf_op jit(solution)/shard_map/psum | solution.py:85
  279.1 1.0 multiply_reduce_fusion.2
  280.1 9.8 %all-reduce.2 = (f32[8]{0:T(128)S(1)}, f32[8]{0:T(128)S(1)}) all-reduce(f32[8]{0:T(128)S(1)} %get-tuple-element.19, f32[8]{0:T(128)S(1)} %get-tuple-element.18), channel_id=1, replica_groups=mesh['var'=8,'samp'=4] {'samp'}, use_global_device_ids=true, to_apply=%region_17.19 | all-reduce | flops 16 | bytes 128 | tf_op jit(solution)/shard_map/psum | solution.py:86
  290.0 0.9 multiply_subtract_fusion.1
  290.9 3.4 convolution_bitcast_fusion.1
  294.3 14.4 %psum.100 = f32[8,8,128]{2,0,1:T(8,128)S(1)} all-reduce(f32[8,8,128]{2,0,1:T(8,128)S(1)} %convolution_bitcast_fusion.1), channel_id=1, replica_groups=mesh['var'=8,'samp'=4] {'samp'}, use_global_device_ids=true, to_apply=%region_20.22 | all-reduce | flops 8192 | bytes 65536 | tf_op jit(solution)/shard_map/psum | solution.py:72
  308.6 8.3 %all_to_all.75 = f32[8,8,128]{2,0,1:T(8,128)S(1)} all-to-all(f32[8,8,128]{2,0,1:T(8,128)S(1)} %psum.100), channel_id=1, replica_groups=mesh['var'=8,'samp'=4] {'var'}, dimensions={1} | all-to-all | bytes 65536 | tf_op jit(solution)/shard_map/all_to_all | solution.py:75
  316.9 0.2 copy.89
  317.1 1.0 gather_fusion.3
  318.3 0.5 convolution_convert_fusion
  318.9 0.2 copy.91
  319.1 1.8 scatter_custom_fusion.2
  320.9 0.7 copy.92
  321.6 3.3 all-to-all-start.5
  325.0 0.3 all-reduce.9.cloned.1.call-start
  325.2 6.3 %convolution_bitcast_fusion = f32[8,2048]{1,0:T(8,128)} fusion(bf16[2048,2048]{0,1:T(8,128)(2,1)} %fusion, f32[8,2048]{1,0:T(8,128)S(1)} %copy-done.2), kind=kOutput, calls=%fused_computation.10 | convolution fusion | flops 67125248 | bytes 8519680 | tf_op jit(solution)/shard_map/dot_general | solution.py:55
  331.6 3.5 fusion.18
  335.1 38.0 %all-reduce.9.cloned.1.call-done = f32[8,2048]{1,0:T(8,128)} async-done(((f32[8,2048]{1,0:T(8,128)}), f32[8,2048]{1,0:T(8,128)}) %all-reduce.9.cloned.1.call-update) | async-done | bytes 65552 | tf_op jit(solution)/shard_map/psum | solution.py:55
  373.1 1.5 broadcast_multiply_fusion
  374.6 55.2 %all-reduce.15.cloned.1.call-done = f32[8,2048]{1,0:T(8,128)} async-done(((f32[8,2048]{1,0:T(8,128)}), f32[8,2048]{1,0:T(8,128)}) %all-reduce.15.cloned.1.call-update) | async-done | bytes 65552 | tf_op jit(solution)/shard_map/psum | solution.py:85
  429.8 1.0 multiply_reduce_fusion
  430.8 9.8 %all-reduce.1 = (f32[8]{0:T(128)S(1)}, f32[8]{0:T(128)S(1)}) all-reduce(f32[8]{0:T(128)S(1)} %get-tuple-element.17, f32[8]{0:T(128)S(1)} %get-tuple-element.16), channel_id=1, replica_groups=mesh['var'=8,'samp'=4] {'samp'}, use_global_device_ids=true, to_apply=%region_24.26 | all-reduce | flops 16 | bytes 128 | tf_op jit(solution)/shard_map/psum | solution.py:86
  440.6 0.7 multiply_add_fusion
  441.3 1.5 multiply_subtract_fusion
  (50 shorter events, 1.3 us)
Async XLA Ops:
  8.0 100.0 %copy-start = (f32[2,256,256]{2,1,0:T(8,128)S(1)}, f32[2,256,256]{2,1,0:T(8,128)}, u32[]{:S(2)}) copy-start(f32[2,256,256]{2,1,0:T(8,128)} %param.15) | copy-start | bytes 1572868
  10.0 12.4 %copy-start.4 = (s32[448]{0:T(512)S(1)}, s32[448]{0:T(512)}, u32[]{:S(2)}) copy-start(s32[448]{0:T(512)} %param.16) | copy-start | bytes 5380
  10.0 12.3 %copy-start.5 = (s32[64]{0:T(128)S(1)}, s32[64]{0:T(128)}, u32[]{:S(2)}) copy-start(s32[64]{0:T(128)} %param.17) | copy-start | bytes 772
  46.5 5.7 %slice-start = ((s8[8388608]{0:T(1024)(128)(4,1)}), s8[4194304]{0:T(1024)(128)(4,1)S(1)}, s32[]{:S(2)}) async-start(s8[8388608]{0:T(1024)(128)(4,1)} %bitcast.131), calls=%async_computation.10 | async-start | bytes 8388608
  47.6 4.6 %slice-start.1 = ((s8[8388608]{0:T(1024)(128)(4,1)}), s8[4194304]{0:T(1024)(128)(4,1)S(1)}, s32[]{:S(2)}) async-start(s8[8388608]{0:T(1024)(128)(4,1)} %bitcast.131), calls=%async_computation.11 | async-start | bytes 8388608
  74.7 4.8 %copy-start.2 = (f32[8,2048]{1,0:T(8,128)S(1)}, f32[8,2048]{1,0:T(8,128)}, u32[]{:S(2)}) copy-start(f32[8,2048]{1,0:T(8,128)} %param.13) | copy-start | bytes 196612
  77.5 2.0 copy-start.1
  79.5 28.5 %copy-start.3 = (f32[8,448]{1,0:T(8,128)S(1)}, f32[8,448]{1,0:T(8,128)}, u32[]{:S(2)}) copy-start(f32[8,448]{1,0:T(8,128)} %param.14) | copy-start | bytes 43012
  97.5 9.1 %all-to-all-start = ((f32[8,8,128]{2,0,1:T(8,128)}), f32[8,8,128]{2,0,1:T(8,128)S(1)}, u32[]{:S(2)}, u32[]{:S(2)}) async-start(f32[8,8,128]{2,0,1:T(8,128)} %psum.92), calls=%async_computation | async-start | bytes 65536 | tf_op jit(solution)/shard_map/all_to_all | solution.py:75
  100.9 72.6 %all-reduce.11.cloned.1.call-start = ((), (), s32[]{:S(2)}) async-start(), calls=%async_computation.7 | async-start | bytes 131072 | tf_op jit(solution)/shard_map/psum | solution.py:85
  122.2 156.9 %all-reduce.13.cloned.1.call-start = ((), (), s32[]{:S(2)}) async-start(), calls=%async_computation.8 | async-start | bytes 131072 | tf_op jit(solution)/shard_map/psum | solution.py:85
  321.6 10.0 %all-to-all-start.5 = ((bf16[8,8,128]{2,0,1:T(8,128)(2,1)}), bf16[8,8,128]{2,0,1:T(8,128)(2,1)S(1)}, u32[]{:S(2)}, u32[]{:S(2)}) async-start(bf16[8,8,128]{2,0,1:T(8,128)(2,1)} %copy.92), calls=%async_computation.5 | async-start | bytes 32768 | tf_op jit(solution)/shard_map/all_to_all | solution.py:81
  325.0 48.1 %all-reduce.9.cloned.1.call-start = ((), (), s32[]{:S(2)}) async-start(), calls=%async_computation.6 | async-start | bytes 131072 | tf_op jit(solution)/shard_map/psum | solution.py:55
  331.5 98.2 %all-reduce.15.cloned.1.call-start = ((), (), s32[]{:S(2)}) async-start(), calls=%async_computation.9 | async-start | bytes 131072 | tf_op jit(solution)/shard_map/psum | solution.py:85
Sparse Core Ops, SparseCore 0:
  122.3 51.1 all-reduce.10
  227.1 52.0 all-reduce.12
Sparse Core Ops, SparseCore 1:
  331.6 41.4 all-reduce.8
  375.3 54.4 all-reduce.14
where the time goes:
time: 452 us; the launch traced here: 450 us
  waiting for transfers between devices  202 us (45%)
  blocking collectives  122 us (27%)
  local copies, waits for them, and re-layouts  43.8 us (10%)
  other arithmetic  31 us (7%)
  matrix products  27.8 us (6%)
  between operations  15.9 us (4%)
  starting transfers between devices  7.27 us (2%)
    psum x3, waiting for transfers between devices, on_device(): update = lax.psum(partial_update, 'var') * inv_root  159 us
    psum x3, blocking collectives, on_device(): lax.psum(jnp.dot(resid_low, selected, preferred_element_type=jnp.float32)...  45.6 us
    psum x1, waiting for transfers between devices, on_device(): lax.psum(jnp.dot(resid_low, dequant, preferred_element_type=jnp.float32),...  38 us
    psum x3, blocking collectives, on_device(): lax.psum((jnp.sum(current * update, 1), jnp.sum(update * update, 1)), 'sa...  29.5 us
    all_to_all x2, blocking collectives, on_device(): lax.all_to_all(partial_sums, 'var', split_axis=1, concat_axis=1, tiled=True)  16.6 us
    all_to_all x2, blocking collectives, on_device(): lax.all_to_all(placed, 'var', split_axis=1, concat_axis=1, tiled=True)  16 us
    all_gather x1, blocking collectives, on_device(): lax.all_gather(local_ids, 'var', axis=0, tiled=True)  14.5 us
    unnamed x17, local copies, waits for them, and re-layouts  14.3 us
  transfers between devices with their start and end apart: 6, of which 5 were waited for; matrix products, arithmetic and copies ran while one was open for 2% of the time, Pallas kernels for 0%

commit v1 on v0

--- a/solution.py
+++ b/solution.py
@@ -69,8 +69,11 @@
     coeffs = jnp.concatenate([beta_active, jnp.zeros((phenos, admit_ids.shape[0]), jnp.float32)], 1)
     current = residual
     for pass_index in range(PASSES):
-        partial_sums = lax.psum(
-            jnp.dot(resid_low, selected, preferred_element_type=jnp.float32), "samp"
+        partial_sums = jnp.sum(
+            lax.all_gather(
+                jnp.dot(resid_low, selected, preferred_element_type=jnp.float32), "samp"
+            ),
+            axis=0,
         )
         routed = lax.all_to_all(partial_sums, "var", split_axis=1, concat_axis=1, tiled=True)
         gradient = jnp.take(routed, position, axis=1) * inv_root

time: 452 us -> 431 us (0.954)
  blocking collectives: 122 us -> 100 us
    psum x3 -> x0, blocking collectives: 45.6 us -> none  [on_device(): lax.psum(jnp.dot(resid_low, selected, preferred_element_type=jnp.float32)...]
    all_gather x0 -> x3, blocking collectives: none -> 23.5 us  [on_device(): lax.all_gather(jnp.dot(resid_low, selected, preferred_element_type=jnp.fl...]
  transfers between devices with their start and end apart: 6 -> 6, of which waited for: 5 -> 5; matrix products, arithmetic and copies ran while one was open for 2% -> 3% of each run, Pallas kernels for 0% -> 0%
where the time goes in v1:
time: 431 us; the launch traced here: 430 us
  waiting for transfers between devices  203 us (47%)
  blocking collectives  100 us (23%)
  local copies, waits for them, and re-layouts  43.8 us (10%)
  other arithmetic  31.6 us (7%)
  matrix products  27.8 us (6%)
  between operations  15.9 us (4%)
  starting transfers between devices  7.27 us (2%)
    psum x3, waiting for transfers between devices, on_device(): update = lax.psum(partial_update, 'var') * inv_root  160 us
    psum x1, waiting for transfers between devices, on_device(): lax.psum(jnp.dot(resid_low, dequant, preferred_element_type=jnp.float32),...  38 us
    psum x3, blocking collectives, on_device(): lax.psum((jnp.sum(current * update, 1), jnp.sum(update * update, 1)), 'sa...  29.5 us
    all_gather x3, blocking collectives, on_device(): lax.all_gather(jnp.dot(resid_low, selected, preferred_element_type=jnp.fl...  23.5 us
    all_to_all x2, blocking collectives, on_device(): lax.all_to_all(partial_sums, 'var', split_axis=1, concat_axis=1, tiled=True)  16.6 us
    all_to_all x2, blocking collectives, on_device(): lax.all_to_all(placed, 'var', split_axis=1, concat_axis=1, tiled=True)  16 us
    all_gather x1, blocking collectives, on_device(): lax.all_gather(local_ids, 'var', axis=0, tiled=True)  14.5 us
    unnamed x17, local copies, waits for them, and re-layouts  14.3 us
  transfers between devices with their start and end apart: 6, of which 5 were waited for; matrix products, arithmetic and copies ran while one was open for 3% of the time, Pallas kernels for 0%

profile of v1, /device:TPU:0, one launch (start us, length us, event | category | flops | bytes accessed | tf_op | source)
XLA Modules:
  0.0 429.7 jit_solution(17546687558954637446)
XLA Ops:
  8.0 1.7 fusion.3
  9.7 0.3 copy.87
  10.1 12.3 %copy.72 = bf16[2048,2048]{0,1:T(8,128)(2,1)} copy(bf16[2048,2048]{1,0:T(8,128)(2,1)} %param.10) | data formatting | bytes 16777216 | tf_op args[0]
  22.5 14.5 %all-gather.3 = s32[8,1,512]{2,1,0:T(1,128)S(1)} all-gather(s32[1,1,512]{2,1,0:T(1,128)S(1)} %bitcast.162), channel_id=1, replica_groups=mesh['var'=8,'samp'=4] {'var'}, dimensions={0}, use_global_device_ids=true | all-gather | bytes 18432 | tf_op jit(solution)/shard_map/all_gather | solution.py:57
  37.0 9.0 %reduce-window.6 = s32[8,8,4,128]{3,1,2,0:T(8,128)S(1)} reduce-window(s32[8,8,4,128]{3,1,2,0:T(8,128)S(1)} %fusion.13, s32[]{:T(128)} %constant.73.clone.1), window={size=1x1x1x128 pad=0_0x0_0x0_0x127_0}, to_apply=%region_1.2 | reduce-window | flops 4161536 | bytes 262148 | tf_op jit(solution)/shard_map/reduce-window
  46.1 0.3 copy.73
  46.7 0.4 fusion.2
  47.1 0.5 select_reduce_fusion
  47.6 4.6 %mul.124 = f32[16,128,2048]{1,0,2:T(8,128)S(1)} broadcast(f32[16,2048]{0,1:T(8,128)S(1)} %bitcast.136), dimensions={0,2} | broadcast | bytes 16908288 | tf_op jit(solution)/shard_map/mul | solution.py:18
  52.2 9.2 %fusion = bf16[2048,2048]{0,1:T(8,128)(2,1)} fusion(f32[256,8,16,128]{3,2,1,0:T(8,128)S(1)} %bitcast.133, bf16[2048,2048]{0,1:T(8,128)(2,1)S(1)} %bitcast.135), kind=kLoop, calls=%fused_computation.8 | loop fusion | flops 12582912 | bytes 33554432 | tf_op jit(solution)/shard_map/convert_element_type | solution.py:21
  61.4 13.3 %gather_fusion = bf16[1024,2048]{1,0:T(8,128)(2,1)} fusion(bf16[2048,2048]{0,1:T(8,128)(2,1)} %fusion, s32[1024]{0:T(1024)S(1)} %broadcast_clamp_fusion), kind=kCustom, calls=%fused_computation.3 | custom fusion | bytes 8392704 | tf_op jit(solution)/shard_map/jit(_take)/gather | solution.py:66
  74.7 2.8 select_select_fusion
  77.5 2.0 copy-done.1
  79.5 1.2 convolution_bitcast_fusion.1
  80.6 8.5 %all-gather = f32[32,1024]{1,0:T(8,128)S(1)} all-gather(f32[8,1024]{1,0:T(8,128)S(1)} %convolution_bitcast_fusion.1), channel_id=2, replica_groups=mesh['var'=8,'samp'=4] {'samp'}, dimensions={0}, use_global_device_ids=true | all-gather | bytes 163840 | tf_op jit(solution)/shard_map/all_gather | solution.py:73
  89.1 0.6 bitcast_reduce_fusion.2
  89.7 3.4 all-to-all-start
  93.1 0.2 all-reduce.11.cloned.1.call-start
  93.4 5.5 %all-to-all-done = f32[8,8,128]{2,0,1:T(8,128)S(1)} async-done(((f32[8,8,128]{2,0,1:T(8,128)}), f32[8,8,128]{2,0,1:T(8,128)S(1)}, u32[]{:S(2)}, u32[]{:S(2)}) %all-to-all-start) | async-done | bytes 32800 | tf_op jit(solution)/shard_map/all_to_all | solution.py:78
  98.8 0.2 copy.75
  99.0 1.0 gather_fusion.1
  100.2 0.5 convolution_convert_fusion.2
  100.7 0.2 copy.77
  100.9 1.8 scatter_custom_fusion
  102.9 8.0 %all_to_all.72 = bf16[8,8,128]{2,0,1:T(8,128)(2,1)S(1)} all-to-all(bf16[8,8,128]{2,0,1:T(8,128)(2,1)S(1)} %copy.78), channel_id=1, replica_groups=mesh['var'=8,'samp'=4] {'var'}, dimensions={1} | all-to-all | bytes 32768 | tf_op jit(solution)/shard_map/all_to_all | solution.py:84
  110.9 3.5 fusion.26
  114.4 52.2 %all-reduce.11.cloned.1.call-done = f32[8,2048]{1,0:T(8,128)} async-done(((f32[8,2048]{1,0:T(8,128)}), f32[8,2048]{1,0:T(8,128)}) %all-reduce.11.cloned.1.call-update) | async-done | bytes 65552 | tf_op jit(solution)/shard_map/psum | solution.py:88
  166.6 1.0 multiply_reduce_fusion.4
  167.6 9.8 %all-reduce.3 = (f32[8]{0:T(128)S(1)}, f32[8]{0:T(128)S(1)}) all-reduce(f32[8]{0:T(128)S(1)} %get-tuple-element.21, f32[8]{0:T(128)S(1)} %get-tuple-element.20), channel_id=1, replica_groups=mesh['var'=8,'samp'=4] {'samp'}, use_global_device_ids=true, to_apply=%region_10.12 | all-reduce | flops 16 | bytes 128 | tf_op jit(solution)/shard_map/psum | solution.py:89
  177.5 0.9 multiply_subtract_fusion.2
  178.4 3.4 fusion.16
  181.8 7.5 %all-gather.1 = f32[32,1024]{1,0:T(8,128)S(1)} all-gather(f32[8,1024]{1,0:T(8,128)S(1)} %fusion.16), channel_id=3, replica_groups=mesh['var'=8,'samp'=4] {'samp'}, dimensions={0}, use_global_device_ids=true | all-gather | bytes 163840 | tf_op jit(solution)/shard_map/all_gather | solution.py:73
  189.3 8.3 %all_to_all.73 = f32[8,8,128]{2,0,1:T(8,128)S(1)} all-to-all(f32[8,8,128]{2,0,1:T(8,128)S(1)} %bitcast.151), channel_id=1, replica_groups=mesh['var'=8,'samp'=4] {'var'}, dimensions={1} | all-to-all | bytes 65536 | tf_op jit(solution)/shard_map/all_to_all | solution.py:78
  197.6 0.2 copy.79
  197.8 1.0 gather_fusion.2
  199.0 0.5 convolution_convert_fusion.1
  199.5 0.2 copy.81
  199.7 1.8 scatter_custom_fusion.1
  201.7 8.0 %all_to_all.74 = bf16[8,8,128]{2,0,1:T(8,128)(2,1)S(1)} all-to-all(bf16[8,8,128]{2,0,1:T(8,128)(2,1)S(1)} %copy.82), channel_id=1, replica_groups=mesh['var'=8,'samp'=4] {'var'}, dimensions={1} | all-to-all | bytes 32768 | tf_op jit(solution)/shard_map/all_to_all | solution.py:84
  209.7 3.5 fusion.23
  213.2 52.2 %all-reduce.13.cloned.1.call-done = f32[8,2048]{1,0:T(8,128)} async-done(((f32[8,2048]{1,0:T(8,128)}), f32[8,2048]{1,0:T(8,128)}) %all-reduce.13.cloned.1.call-update) | async-done | bytes 65552 | tf_op jit(solution)/shard_map/psum | solution.py:88
  265.4 1.0 multiply_reduce_fusion.2
  266.4 9.8 %all-reduce.2 = (f32[8]{0:T(128)S(1)}, f32[8]{0:T(128)S(1)}) all-reduce(f32[8]{0:T(128)S(1)} %get-tuple-element.19, f32[8]{0:T(128)S(1)} %get-tuple-element.18), channel_id=1, replica_groups=mesh['var'=8,'samp'=4] {'samp'}, use_global_device_ids=true, to_apply=%region_17.19 | all-reduce | flops 16 | bytes 128 | tf_op jit(solution)/shard_map/psum | solution.py:89
  276.2 0.9 multiply_subtract_fusion.1
  277.1 3.4 fusion.14
  280.5 7.5 %all-gather.2 = f32[32,1024]{1,0:T(8,128)S(1)} all-gather(f32[8,1024]{1,0:T(8,128)S(1)} %fusion.14), channel_id=4, replica_groups=mesh['var'=8,'samp'=4] {'samp'}, dimensions={0}, use_global_device_ids=true | all-gather | bytes 163840 | tf_op jit(solution)/shard_map/all_gather | solution.py:73
  288.0 8.3 %all_to_all.75 = f32[8,8,128]{2,0,1:T(8,128)S(1)} all-to-all(f32[8,8,128]{2,0,1:T(8,128)S(1)} %bitcast.152), channel_id=1, replica_groups=mesh['var'=8,'samp'=4] {'var'}, dimensions={1} | all-to-all | bytes 65536 | tf_op jit(solution)/shard_map/all_to_all | solution.py:78
  296.3 0.2 copy.83
  296.5 1.0 gather_fusion.3
  297.7 0.5 convolution_convert_fusion
  298.3 0.2 copy.85
  298.5 1.8 scatter_custom_fusion.2
  300.3 0.7 copy.86
  301.0 3.3 all-to-all-start.5
  304.4 0.3 all-reduce.9.cloned.1.call-start
  304.6 6.3 %convolution_bitcast_fusion = f32[8,2048]{1,0:T(8,128)} fusion(bf16[2048,2048]{0,1:T(8,128)(2,1)} %fusion, f32[8,2048]{1,0:T(8,128)S(1)} %copy-done.2), kind=kOutput, calls=%fused_computation.10 | convolution fusion | flops 67125248 | bytes 8519680 | tf_op jit(solution)/shard_map/dot_general | solution.py:55
  311.0 3.5 fusion.20
  314.5 38.0 %all-reduce.9.cloned.1.call-done = f32[8,2048]{1,0:T(8,128)} async-done(((f32[8,2048]{1,0:T(8,128)}), f32[8,2048]{1,0:T(8,128)}) %all-reduce.9.cloned.1.call-update) | async-done | bytes 65552 | tf_op jit(solution)/shard_map/psum | solution.py:55
  352.5 1.5 broadcast_multiply_fusion
  354.0 55.2 %all-reduce.15.cloned.1.call-done = f32[8,2048]{1,0:T(8,128)} async-done(((f32[8,2048]{1,0:T(8,128)}), f32[8,2048]{1,0:T(8,128)}) %all-reduce.15.cloned.1.call-update) | async-done | bytes 65552 | tf_op jit(solution)/shard_map/psum | solution.py:88
  409.2 1.0 multiply_reduce_fusion
  410.2 9.8 %all-reduce.1 = (f32[8]{0:T(128)S(1)}, f32[8]{0:T(128)S(1)}) all-reduce(f32[8]{0:T(128)S(1)} %get-tuple-element.17, f32[8]{0:T(128)S(1)} %get-tuple-element.16), channel_id=1, replica_groups=mesh['var'=8,'samp'=4] {'samp'}, use_global_device_ids=true, to_apply=%region_24.26 | all-reduce | flops 16 | bytes 128 | tf_op jit(solution)/shard_map/psum | solution.py:89
  420.1 0.7 multiply_add_fusion
  420.8 1.5 multiply_subtract_fusion
  (53 shorter events, 1.4 us)
Async XLA Ops:
  8.0 92.2 %copy-start = (f32[2,256,256]{2,1,0:T(8,128)S(1)}, f32[2,256,256]{2,1,0:T(8,128)}, u32[]{:S(2)}) copy-start(f32[2,256,256]{2,1,0:T(8,128)} %param.15) | copy-start | bytes 1572868
  10.0 12.4 %copy-start.4 = (s32[448]{0:T(512)S(1)}, s32[448]{0:T(512)}, u32[]{:S(2)}) copy-start(s32[448]{0:T(512)} %param.16) | copy-start | bytes 5380
  10.0 12.3 %copy-start.5 = (s32[64]{0:T(128)S(1)}, s32[64]{0:T(128)}, u32[]{:S(2)}) copy-start(s32[64]{0:T(128)} %param.17) | copy-start | bytes 772
  46.5 5.7 %slice-start = ((s8[8388608]{0:T(1024)(128)(4,1)}), s8[4194304]{0:T(1024)(128)(4,1)S(1)}, s32[]{:S(2)}) async-start(s8[8388608]{0:T(1024)(128)(4,1)} %bitcast.134), calls=%async_computation.10 | async-start | bytes 8388608
  47.6 4.6 %slice-start.1 = ((s8[8388608]{0:T(1024)(128)(4,1)}), s8[4194304]{0:T(1024)(128)(4,1)S(1)}, s32[]{:S(2)}) async-start(s8[8388608]{0:T(1024)(128)(4,1)} %bitcast.134), calls=%async_computation.11 | async-start | bytes 8388608
  74.7 4.8 %copy-start.2 = (f32[8,2048]{1,0:T(8,128)S(1)}, f32[8,2048]{1,0:T(8,128)}, u32[]{:S(2)}) copy-start(f32[8,2048]{1,0:T(8,128)} %param.13) | copy-start | bytes 196612
  77.5 2.0 copy-start.1
  79.5 20.7 %copy-start.3 = (f32[8,448]{1,0:T(8,128)S(1)}, f32[8,448]{1,0:T(8,128)}, u32[]{:S(2)}) copy-start(f32[8,448]{1,0:T(8,128)} %param.14) | copy-start | bytes 43012
  89.7 9.1 %all-to-all-start = ((f32[8,8,128]{2,0,1:T(8,128)}), f32[8,8,128]{2,0,1:T(8,128)S(1)}, u32[]{:S(2)}, u32[]{:S(2)}) async-start(f32[8,8,128]{2,0,1:T(8,128)} %bitcast.17), calls=%async_computation | async-start | bytes 65536 | tf_op jit(solution)/shard_map/all_to_all | solution.py:78
  93.1 73.5 %all-reduce.11.cloned.1.call-start = ((), (), s32[]{:S(2)}) async-start(), calls=%async_computation.7 | async-start | bytes 131072 | tf_op jit(solution)/shard_map/psum | solution.py:88
  114.4 151.0 %all-reduce.13.cloned.1.call-start = ((), (), s32[]{:S(2)}) async-start(), calls=%async_computation.8 | async-start | bytes 131072 | tf_op jit(solution)/shard_map/psum | solution.py:88
  301.0 10.0 %all-to-all-start.5 = ((bf16[8,8,128]{2,0,1:T(8,128)(2,1)}), bf16[8,8,128]{2,0,1:T(8,128)(2,1)S(1)}, u32[]{:S(2)}, u32[]{:S(2)}) async-start(bf16[8,8,128]{2,0,1:T(8,128)(2,1)} %copy.86), calls=%async_computation.5 | async-start | bytes 32768 | tf_op jit(solution)/shard_map/all_to_all | solution.py:84
  304.4 48.2 %all-reduce.9.cloned.1.call-start = ((), (), s32[]{:S(2)}) async-start(), calls=%async_computation.6 | async-start | bytes 131072 | tf_op jit(solution)/shard_map/psum | solution.py:55
  310.9 98.3 %all-reduce.15.cloned.1.call-start = ((), (), s32[]{:S(2)}) async-start(), calls=%async_computation.9 | async-start | bytes 131072 | tf_op jit(solution)/shard_map/psum | solution.py:88
Sparse Core Ops, SparseCore 0:
  114.5 52.0 all-reduce.10
  213.3 52.0 all-reduce.12
Sparse Core Ops, SparseCore 1:
  311.0 41.5 all-reduce.8
  354.7 54.4 all-reduce.14
